TPU v7x, 32 devices: a whole 2x2x4 slice. The times are simulated.
32 devices in a mesh: expert: 8 (over z, x), tensor: 4 (over y, core).
Axes of the slice: x: 2, y: 2, z: 4, core: 2. Of those that a mesh axis runs over, the one named last changes fastest.
Arguments:
- tokens: bfloat16 [1024, 3584], P('expert', 'tensor'), may hold values from -6 to 6
- expert_ids: int32 [1024, 4], P('expert'), may hold values from 0 to 7, all different within a row; in each aligned block of 128 rows (0 to 127, 128 to 255, ...) at most 96 rows name the same one
- gate_values: bfloat16 [1024, 4], P('expert'), may hold values from 0.049804688 to 0.3984375
- w_gate: bfloat16 [8, 3584, 1024], P('expert', None, 'tensor'), may hold values from -0.09375 to 0.09375
- w_up: bfloat16 [8, 3584, 1024], P('expert', None, 'tensor'), may hold values from -0.09375 to 0.09375
- w_down: bfloat16 [8, 1024, 3584], P('expert', 'tensor'), may hold values from -0.1875 to 0.1875
- shared_gate: bfloat16 [3584, 1024], P(None, 'tensor'), may hold values from -0.09375 to 0.09375
- shared_up: bfloat16 [3584, 1024], P(None, 'tensor'), may hold values from -0.09375 to 0.09375
- shared_down: bfloat16 [1024, 3584], P('tensor'), may hold values from -0.1875 to 0.1875
Outputs:
- moe_output: bfloat16 [1024, 3584], P('expert', 'tensor')
Inputs may be any that keep to these rules, and one draw needn't show every extreme that they name: `expert_ids`: each token names 4 different experts. Among the 128 tokens of one index of the expert axis (aligned blocks of 128 rows) no expert is named by more than 96 tokens, a bound that some block reaches.
All inputs are finite; a program needn't handle non-finite values.
Results may differ from a plain program's by a relative error of at most 0.013.
Values may be sent and summed in bfloat16 or wider, within the bound.
A program may use at most 64 MiB of HBM per device.

v0:
```python
import jax
import jax.numpy as jnp
from jax import lax
from jax.sharding import PartitionSpec as P


def per_device(
    tokens, expert_ids, gate_values, w_gate, w_up, w_down, shared_gate, shared_up, shared_down
):
    tok_dev, narrow = tokens.shape
    top_count = expert_ids.shape[1]
    per_lane, features, quarter = w_gate.shape
    lane_count = lax.axis_size("expert")
    experts_all = lane_count * per_lane
    capacity = min(tok_dev, 3 * tok_dev * top_count // (2 * experts_all))
    total_rows = experts_all * capacity
    numbers = jnp.arange(experts_all, dtype=jnp.int32)
    onehot = (expert_ids[:, :, None] == numbers).astype(jnp.int32)
    per_token = jnp.sum(onehot, axis=1)
    earlier = jnp.cumsum(per_token, axis=0) - per_token
    slot_index = jnp.sum(onehot * earlier[:, None, :], axis=2)
    target = expert_ids * capacity + slot_index
    token_index = jnp.repeat(jnp.arange(tok_dev, dtype=jnp.int32), top_count)
    owners = jnp.full((total_rows,), tok_dev, jnp.int32).at[target.reshape(-1)].set(token_index)
    features_all = lax.all_gather(tokens, "tensor", axis=1, tiled=True)
    shared_gate_sums = jnp.dot(features_all, shared_gate, preferred_element_type=jnp.float32)
    shared_up_sums = jnp.dot(features_all, shared_up, preferred_element_type=jnp.float32)
    shared_hidden = (jax.nn.silu(shared_gate_sums) * shared_up_sums).astype(jnp.bfloat16)
    shared_partial = jnp.dot(shared_hidden, shared_down, preferred_element_type=jnp.float32)
    padded = jnp.concatenate([tokens, jnp.zeros((1, narrow), jnp.bfloat16)], axis=0)
    outgoing = padded[owners].reshape(lane_count, per_lane * capacity, narrow)
    arrived = lax.all_to_all(outgoing, "expert", split_axis=0, concat_axis=0, tiled=True)
    arrived = arrived.reshape(lane_count, per_lane, capacity, narrow)
    block_rows = lax.all_gather(arrived, "tensor", axis=3, tiled=True)
    gate_more = jnp.einsum("sjcd,jdf->sjcf", block_rows, w_gate, preferred_element_type=jnp.float32)
    up_more = jnp.einsum("sjcd,jdf->sjcf", block_rows, w_up, preferred_element_type=jnp.float32)
    hidden = (jax.nn.silu(gate_more) * up_more).astype(jnp.bfloat16)
    partial_value = jnp.einsum("sjcf,jfd->sjcd", hidden, w_down, preferred_element_type=jnp.float32)
    summed = lax.psum_scatter(
        partial_value.astype(jnp.bfloat16), "tensor", scatter_dimension=3, tiled=True
    ).astype(jnp.float32)
    returned = lax.all_to_all(
        summed.reshape(lane_count, per_lane * capacity, narrow).astype(jnp.bfloat16),
        "expert",
        split_axis=0,
        concat_axis=0,
        tiled=True,
    ).astype(jnp.float32)
    picked = returned.reshape(total_rows, narrow)[target]
    routed = jnp.sum(gate_values.astype(jnp.float32)[:, :, None] * picked, axis=1)
    shared_total = lax.psum_scatter(
        shared_partial.astype(jnp.bfloat16), "tensor", scatter_dimension=1, tiled=True
    ).astype(jnp.float32)
    return (routed + shared_total).astype(jnp.bfloat16)


def solution(mesh):
    placed = (
        P("expert", "tensor"),
        P("expert", None),
        P("expert", None),
        P("expert", None, "tensor"),
        P("expert", None, "tensor"),
        P("expert", "tensor", None),
        P(None, "tensor"),
        P(None, "tensor"),
        P("tensor", None),
    )
    return jax.shard_map(
        per_device, mesh=mesh, in_specs=placed, out_specs=P("expert", "tensor"), check_vma=False
    )
```

profile of v0, /device:TPU:0, one launch (start us, length us, event | category | flops | bytes accessed | tf_op | source)
XLA Modules:
  0.0 257.3 jit_solution(4666250185301793494)
XLA Ops:
  6.5 0.8 convert_reduce_fusion
  7.5 0.2 reduce_window_sum.11
  7.7 0.7 select_reduce_fusion
  8.4 0.7 compare_select_fusion.2
  9.1 0.1 copy.24
  9.5 2.4 scatter_custom_fusion
  11.9 1.0 concatenate.3
  12.9 2.8 %gather_fusion = bf16[768,896]{1,0:T(8,128)(2,1)S(1)} fusion(bf16[129,896]{1,0:T(8,128)(2,1)S(1)} %concatenate.3, s32[1024]{0:T(1024)S(1)} %pad_clamp_fusion.1), kind=kCustom, calls=%fused_computation | custom fusion | bytes 2755584 | tf_op jit(solution)/shard_map/gather | solution.py:31
  15.7 40.6 %all_to_all.10 = bf16[8,96,896]{2,1,0:T(8,128)(2,1)} all-to-all(bf16[8,96,896]{2,1,0:T(8,128)(2,1)S(1)} %bitcast.77), channel_id=1, replica_groups=mesh['expert'=8,'tensor'=4] {'expert'}, dimensions={0} | all-to-all | bytes 2752512 | tf_op jit(solution)/shard_map/all_to_all | solution.py:32
  56.4 40.4 %all-gather.3.cloned.1.call-done = bf16[8,96,3584]{2,1,0:T(8,128)(2,1)} async-done(((bf16[8,96,896]{2,1,0:T(8,128)(2,1)}), bf16[8,96,3584]{2,1,0:T(8,128)(2,1)}) %all-gather.3.cloned.1.call-update) | async-done | bytes 5505040 | tf_op jit(solution)/shard_map/all_gather | solution.py:34
  96.8 4.7 %fusion.6 = f32[8,1,96,256]{3,2,0,1:T(8,128)S(1)} fusion(bf16[8,96,3584]{2,1,0:T(8,128)(2,1)} %all-gather.3.cloned.1.call-done, bf16[1,3584,256]{2,1,0:T(8,128)(2,1)} %param.12), kind=kOutput, calls=%fused_computation.13 | convolution fusion | flops 1409286144 | bytes 8126464 | tf_op jit(solution)/shard_map/sjcd,jdf->sjcf/dot_general | solution.py:35
  101.5 11.3 %fusion = bf16[8,1,96,3584]{3,2,0,1:T(8,128)(2,1)} fusion(bf16[1,256,3584]{2,1,0:T(8,128)(2,1)S(1)} %copy-done, bf16[8,96,3584]{2,1,0:T(8,128)(2,1)} %all-gather.3.cloned.1.call-done, bf16[1,3584,256]{2,1,0:T(8,128)(2,1)} %param.13, f32[8,1,96,256]{3,2,0,1:T(8,128)S(1)} %fusion.6), kind=kOutput, calls=%fused_computation.4 | convolution fusion | flops 2822504448 | bytes 15466496 | tf_op jit(solution)/shard_map/sjcf,jfd->sjcd/dot_general | solution.py:38
  112.8 10.0 %copy.26 = bf16[8,1,96,3584]{2,0,1,3:T(8,128)(2,1)} copy(bf16[8,1,96,3584]{3,2,0,1:T(8,128)(2,1)} %fusion) | data formatting | bytes 11010048
  122.8 12.3 %reshape.124 = bf16[3584,768]{1,0:T(8,128)(2,1)} reshape(bf16[3584,1,8,96]{3,2,1,0:T(8,128)(2,1)} %bitcast.74) | data formatting | bytes 11010048
  135.1 0.9 copy-done.1
  136.0 9.4 %all_gather.7 = bf16[128,3584]{1,0:T(8,128)(2,1)S(1)} all-gather(bf16[128,896]{1,0:T(8,128)(2,1)S(1)} %copy-done.1), channel_id=1, replica_groups=mesh['expert'=8,'tensor'=4] {'tensor'}, dimensions={1}, use_global_device_ids=true | all-gather | bytes 1146880 | tf_op jit(solution)/shard_map/all_gather | solution.py:25
  145.4 42.9 %reduce-scatter.7.cloned.1.call-done = bf16[896,768]{1,0:T(8,128)(2,1)} async-done(((bf16[3584,768]{1,0:T(8,128)(2,1)}), bf16[896,768]{1,0:T(8,128)(2,1)}) %reduce-scatter.7.cloned.1.call-update) | async-done | bytes 1376272
  188.3 4.5 %reshape.125 = bf16[896,1,8,96]{3,2,1,0:T(8,128)(2,1)} reshape(bf16[896,768]{1,0:T(8,128)(2,1)} %reduce-scatter.7.cloned.1.call-done) | data formatting | bytes 2752512
  192.8 3.8 %copy.27 = bf16[8,1,96,896]{3,2,0,1:T(8,128)(2,1)} copy(bf16[8,1,96,896]{2,0,1,3:T(8,128)(2,1)} %bitcast.75) | data formatting | bytes 2752512
  196.6 5.5 %all-to-all-start.1 = ((bf16[8,96,896]{2,1,0:T(8,128)(2,1)}), bf16[8,96,896]{2,1,0:T(8,128)(2,1)}, u32[]{:S(2)}, u32[]{:S(2)}) async-start(bf16[8,96,896]{2,1,0:T(8,128)(2,1)} %bitcast.76), calls=%async_computation.1 | async-start | bytes 2752512 | tf_op jit(solution)/shard_map/all_to_all | solution.py:42
  202.1 0.2 reduce-scatter.9.cloned.1.call-start
  202.3 1.9 fusion.35
  204.2 4.2 %convolution_convert_fusion.1 = bf16[128,3584]{1,0:T(8,128)(2,1)} fusion(bf16[256,3584]{1,0:T(8,128)(2,1)} %param.17, bf16[128,3584]{1,0:T(8,128)(2,1)S(1)} %all_gather.7, bf16[3584,256]{1,0:T(8,128)(2,1)} %param.16, f32[128,256]{1,0:T(8,128)S(1)} %fusion.35), kind=kOutput, calls=%fused_computation.5 | convolution fusion | flops 470417408 | bytes 5636096 | tf_op jit(solution)/shard_map/dot_general | solution.py:29
  208.5 2.2 copy.28
  210.9 0.1 copy.20
  211.1 24.1 %reduce-scatter.9.cloned.1.call-done = bf16[896,128]{1,0:T(8,128)(2,1)} async-done(((bf16[3584,128]{1,0:T(8,128)(2,1)}), bf16[896,128]{1,0:T(8,128)(2,1)}) %reduce-scatter.9.cloned.1.call-update) | async-done | bytes 229392
  235.2 1.1 copy.29
  236.3 3.1 %bitcast_convert_fusion = f32[768,896]{1,0:T(8,128)} fusion(bf16[8,96,896]{2,1,0:T(8,128)(2,1)} %all-to-all-done.1), kind=kLoop, calls=%fused_computation.12 | loop fusion | flops 688128 | bytes 4128768 | tf_op jit(solution)/shard_map/reshape | solution.py:49
  239.4 5.1 %gather_fusion.1 = f32[512,896]{1,0:T(8,128)} fusion(f32[768,896]{1,0:T(8,128)} %bitcast_convert_fusion, s32[1024]{0:T(1024)S(1)} %pad_clamp_fusion), kind=kCustom, calls=%fused_computation.1 | custom fusion | bytes 3672064 | tf_op jit(solution)/shard_map/gather | solution.py:49
  244.5 2.8 %reshape.101 = f32[128,4,896]{2,1,0:T(4,128)} reshape(f32[512,896]{1,0:T(8,128)} %gather_fusion.1) | data formatting | bytes 3670016 | tf_op jit(solution)/shard_map/gather | solution.py:49
  247.3 2.7 %multiply_reduce_fusion = f32[128,896]{1,0:T(8,128)S(1)} fusion(f32[128,4,896]{2,1,0:T(4,128)} %reshape.101, f32[128,4]{1,0:T(8,128)S(1)} %copy.20), kind=kLoop, calls=%fused_computation.11 | loop fusion | flops 802816 | bytes 2295808 | tf_op jit(solution)/shard_map/reduce_sum | solution.py:50
  250.0 0.7 add_convert_fusion
  (23 shorter events, 0.7 us)
Async XLA Ops:
  6.5 95.0 %copy-start = (bf16[1,256,3584]{2,1,0:T(8,128)(2,1)S(1)}, bf16[1,256,3584]{2,1,0:T(8,128)(2,1)}, u32[]{:S(2)}) copy-start(bf16[1,256,3584]{2,1,0:T(8,128)(2,1)} %param.14) | copy-start | bytes 5505028
  6.5 90.2 %all-gather.3.cloned.1.call-start = ((), (), s32[]{:S(2)}) async-start(), calls=%async_computation.4 | async-start | bytes 6881280 | tf_op jit(solution)/shard_map/all_gather | solution.py:34
  56.3 131.9 %reduce-scatter.7.cloned.1.call-start = ((), (), s32[]{:S(2)}) async-start(), calls=%async_computation.5 | async-start | bytes 6881280
  135.1 0.9 copy-start.1
  196.6 39.7 %all-to-all-start.1 = ((bf16[8,96,896]{2,1,0:T(8,128)(2,1)}), bf16[8,96,896]{2,1,0:T(8,128)(2,1)}, u32[]{:S(2)}, u32[]{:S(2)}) async-start(bf16[8,96,896]{2,1,0:T(8,128)(2,1)} %bitcast.76), calls=%async_computation.1 | async-start | bytes 2752512 | tf_op jit(solution)/shard_map/all_to_all | solution.py:42
  202.1 33.1 %reduce-scatter.9.cloned.1.call-start = ((), (), s32[]{:S(2)}) async-start(), calls=%async_computation.6 | async-start | bytes 1146880
  208.5 2.5 copy-start.2
Sparse Core Ops, SparseCore 0:
  56.4 40.2 all-gather.2
  135.2 53.0 reduce-scatter.6
  210.8 24.3 reduce-scatter.8
where the time goes:
time: 258 us; the launch traced here: 257 us
  waiting for transfers between devices  107 us (41%)
  blocking collectives  49.9 us (19%)
  local copies, waits for them, and re-layouts  49.8 us (19%)
  matrix products  22.1 us (9%)
  between operations  13.2 us (5%)
  other arithmetic  8.93 us (3%)
  starting transfers between devices  5.77 us (2%)
    unnamed x5, waiting for transfers between devices  67.1 us
    all_to_all x1, blocking collectives, per_device(): lax.all_to_all(outgoing, 'expert', split_axis=0, concat_axis=0, tiled=True)  40.6 us
    all_gather x1, waiting for transfers between devices, per_device(): block_rows = lax.all_gather(arrived, 'tensor', axis=3, tiled=True)  40.4 us
    unnamed x12, local copies, waits for them, and re-layouts  34.9 us
    dot_general x1, matrix products, per_device(): jnp.einsum('sjcf,jfd->sjcd', hidden, w_down, preferred_element_type=jnp.f...  11.3 us
    all_gather x1, blocking collectives, per_device(): features_all = lax.all_gather(tokens, 'tensor', axis=1, tiled=True)  9.36 us
    gather x2, local copies, waits for them, and re-layouts, per_device(): picked = returned.reshape(total_rows, narrow)[target]  7.93 us
    all_to_all x1, starting transfers between devices, per_device(): lax.all_to_all(summed.reshape(lane_count, per_lane * capacity, narrow).as...  5.51 us
  transfers between devices with their start and end apart: 4, of which 3 were waited for; matrix products, arithmetic and copies ran while one was open for 4% of the time, Pallas kernels for 0%

commit v1 on v0

--- a/solution.py
+++ b/solution.py
@@ -1,10 +1,22 @@
+import functools
+
 import jax
 import jax.numpy as jnp
 from jax import lax
+from jax.experimental import pallas as pl
+from jax.experimental.pallas import tpu as pltpu
 from jax.sharding import PartitionSpec as P
 
-
-def per_device(
+MESH = pl.DeviceIdType.MESH
+F32 = jnp.float32
+BF16 = jnp.bfloat16
+
+
+def capacity_of(tok_dev, top_count, experts_all):
+    return min(tok_dev, 3 * tok_dev * top_count // (2 * experts_all))
+
+
+def dispatch_form(
     tokens, expert_ids, gate_values, w_gate, w_up, w_down, shared_gate, shared_up, shared_down
 ):
     tok_dev, narrow = tokens.shape
@@ -54,6 +66,290 @@
     return (routed + shared_total).astype(jnp.bfloat16)
 
 
+def layer_kernel(
+    lanes, tok_hbm, wt_hbm, wg_hbm, wu_hbm, wd_hbm, sg_hbm, su_hbm, sd_hbm, out_ref,
+    xbuf, wtb, wg, wu, wd, sg, su, sd, shared_hidden, part, got_core, got_h0, got_h1,
+    got_x, got_y, got_z, load_sem, send_sem, recv_sem,
+):
+    planes = lanes // 2
+    rows, narrow = out_ref.shape
+    half, both = rows // 2, 2 * rows
+    quarter = wg.shape[1]
+    lane, tens = lax.axis_index("expert"), lax.axis_index("tensor")
+    z, x = lane // 2, lax.rem(lane, 2)
+    y, c = tens // 2, lax.rem(tens, 2)
+    ox, oy, oc = 1 - x, 1 - y, 1 - c
+    up = lax.rem(z + 1, planes)
+    down = lax.rem(z + planes - 1, planes)
+    at_core = (lane, y * 2 + oc)
+    at_x = (z * 2 + ox, tens)
+    at_y = (lane, oy * 2 + c)
+    at_up = (up * 2 + x, tens)
+    at_down = (down * 2 + x, tens)
+    tens_y = oy * 2 + c
+    number, copies = {}, {}
+
+    def send(key, src, dst, device):
+        k = number.setdefault(key, len(number))
+        copies[key] = pltpu.make_async_remote_copy(
+            src_ref=src, dst_ref=dst, send_sem=send_sem.at[k], recv_sem=recv_sem.at[k],
+            device_id=device, device_id_type=MESH)
+        copies[key].start()
+
+    def arrived(key):
+        copies[key].wait_recv()
+
+    def span(start, size):
+        return pl.ds(pl.multiple_of(start, size), size)
+
+    def piece(t, plane, ix):
+        return xbuf.at[t, span((plane * 2 + ix) * rows, rows), :]
+
+    def half_piece(t, plane, ix, h):
+        return xbuf.at[t, span((plane * 2 + ix) * rows + h * half, half), :]
+
+    loads = []
+    for src, dst in (
+        (tok_hbm, piece(tens, z, x)), (wt_hbm, wtb.at[lane]), (wg_hbm, wg), (wu_hbm, wu),
+        (sg_hbm, sg), (su_hbm, su), (wd_hbm, wd), (sd_hbm, sd),
+    ):
+        copy = pltpu.make_async_copy(src, dst, load_sem.at[len(loads)])
+        copy.start()
+        loads.append(copy)
+
+    barrier = pltpu.get_barrier_semaphore()
+    for device in (at_core, at_x, at_y, at_up, at_down):
+        pl.semaphore_signal(barrier, inc=1, device_id=device, device_id_type=MESH)
+    pl.semaphore_wait(barrier, 5)
+
+    def plane_at(s):
+        return lax.rem(z - s + planes, planes)
+
+    def issue(s):
+        p = plane_at(s)
+        if s == 0:
+            loads[0].wait()
+            loads[1].wait()
+        else:
+            arrived(("z", s - 1))
+            arrived(("wz", s - 1))
+        mine, weight = piece(tens, p, x), wtb.at[p * 2 + x]
+        if s < planes - 1:
+            send(("z", s), mine, mine, at_up)
+            send(("wz", s), weight, weight, at_up)
+        send(("x", s), mine, mine, at_x)
+        send(("y", s), mine, mine, at_y)
+        send(("wx", s), weight, weight, at_x)
+        send(("c", s), mine, mine, at_core)
+
+    def forward(s):
+        p = plane_at(s)
+        arrived(("x", s))
+        first = half_piece(tens, p, ox, 0)
+        send(("d0", s), first, first, at_y)
+        other = piece(tens, p, ox)
+        send(("cx", s), other, other, at_core)
+        arrived(("y", s))
+        second = half_piece(tens_y, p, x, 1)
+        send(("d1", s), second, second, at_x)
+        other = piece(tens_y, p, x)
+        send(("cy", s), other, other, at_core)
+
+    def finish(s):
+        p = plane_at(s)
+        arrived(("d0", s))
+        arrived(("d1", s))
+        far = piece(tens_y, p, ox)
+        send(("cd", s), far, far, at_core)
+        arrived(("wx", s))
+        for key in ("c", "cx", "cy", "cd"):
+            arrived((key, s))
+
+    tensors = xbuf.shape[0]
+
+    def hidden_of(start, count, gate_matrix, up_matrix):
+        gate_sums = up_sums = None
+        for t in range(tensors):
+            block = xbuf[t, span(start, count), :]
+            g = jnp.dot(block, gate_matrix[t * narrow:(t + 1) * narrow, :], preferred_element_type=F32)
+            u = jnp.dot(block, up_matrix[t * narrow:(t + 1) * narrow, :], preferred_element_type=F32)
+            gate_sums = g if t == 0 else gate_sums + g
+            up_sums = u if t == 0 else up_sums + u
+        return gate_sums / (1.0 + jnp.exp(-gate_sums)) * up_sums
+
+    def compute(s):
+        p = plane_at(s)
+        if s == 0:
+            for copy in loads[2:]:
+                copy.wait()
+            shared_hidden[...] = jnp.zeros_like(shared_hidden)
+            shared_hidden[span(x * rows, rows), :] = hidden_of(lane * rows, rows, sg, su).astype(BF16)
+        hidden = hidden_of(p * both, both, wg, wu)
+        picks = lax.broadcasted_iota(jnp.int32, (wtb.shape[1], quarter), 0) == lane
+        picks = picks.astype(F32).astype(BF16)
+        weight = jnp.concatenate([
+            lax.dot_general(wtb[p * 2 + i], picks, (((0,), (0,)), ((), ())), preferred_element_type=F32)
+            for i in range(2)], axis=0)
+        hidden = (hidden * weight).astype(BF16)
+        for t in range(tensors):
+            columns = slice(t * narrow, (t + 1) * narrow)
+            value = jnp.dot(hidden, wd[:, columns], preferred_element_type=F32)
+            if s == 0:
+                value += jnp.dot(shared_hidden[...], sd[:, columns], preferred_element_type=F32)
+            part[s, t] = value.astype(BF16)
+
+    def add(count, dst, *sources):
+        chunk = 32
+
+        def step(i, carry):
+            at = span(i * chunk, chunk)
+            value = dst[at, :].astype(F32)
+            for source in sources:
+                value += source[at, :].astype(F32)
+            dst[at, :] = value.astype(BF16)
+            return carry
+
+        lax.fori_loop(0, count // chunk, step, 0)
+
+    def sum_piece(s, iy, ix):
+        return part.at[s, iy * 2 + c, span(ix * rows, rows), :]
+
+    def reduce_core(s):
+        for i, iy in enumerate((oy, y)):
+            send(("rc", i, s), part.at[s, iy * 2 + oc], got_core.at[s, iy], at_core)
+
+    def reduce_far(s):
+        for i in range(2):
+            arrived(("rc", i, s))
+
+        def side(iy, ix):
+            add(rows, sum_piece(s, iy, ix), got_core.at[s, iy, span(ix * rows, rows), :])
+
+        side(oy, ox)
+        far = sum_piece(s, oy, ox)
+        send(("r0", s), far.at[0:half, :], got_h0.at[s], at_y)
+        send(("r1", s), far.at[half:rows, :], got_h1.at[s], at_x)
+        side(y, ox)
+        side(oy, x)
+        side(y, x)
+
+    def reduce_near(s):
+        arrived(("r0", s))
+        aside = sum_piece(s, y, ox)
+        add(half, aside.at[0:half, :], got_h0.at[s])
+        send(("rx", s), aside, got_x.at[s], at_x)
+        arrived(("r1", s))
+        across = sum_piece(s, oy, x)
+        add(half, across.at[half:rows, :], got_h1.at[s])
+        send(("ry", s), across, got_y.at[s], at_y)
+
+    def reduce_ring(s, before):
+        arrived(("rx", s))
+        arrived(("ry", s))
+        own = sum_piece(s, y, x)
+        sources = [got_x.at[s], got_y.at[s]]
+        if before is not None:
+            arrived(("rz", before))
+            sources.append(got_z.at[before])
+        add(rows, own, *sources)
+        if s == 0:
+            out_ref[...] = own[...]
+        else:
+            send(("rz", s), own, got_z.at[s], at_up)
+
+    last = planes - 1
+    issue(0)
+    forward(0)
+    if last:
+        issue(1)
+    finish(0)
+    compute(0)
+    reduce_core(0)
+    for s in range(1, planes):
+        forward(s)
+        if s < last:
+            issue(s + 1)
+        if s >= 2:
+            reduce_far(s - 1)
+        if s >= 3:
+            reduce_near(s - 2)
+        finish(s)
+        compute(s)
+        reduce_core(s)
+    for s in range(max(1, last - 1), planes):
+        if s == last:
+            reduce_far(s)
+            reduce_far(0)
+        if s == last - 1:
+            reduce_near(s)
+    done = None
+    for s in range(1, last):
+        reduce_ring(s, done)
+        done = s
+    reduce_near(last)
+    reduce_near(0)
+    reduce_ring(last, done)
+    reduce_ring(0, last)
+    for copy in copies.values():
+        copy.wait_send()
+
+
+def kernel_form(
+    tokens, expert_ids, gate_values, w_gate, w_up, w_down, shared_gate, shared_up, shared_down
+):
+    rows, narrow = tokens.shape
+    unused, features, quarter = w_gate.shape
+    lanes, tensors = lax.axis_size("expert"), lax.axis_size("tensor")
+    planes = lanes // 2
+    table = -(-lanes // 16) * 16
+    numbers = jnp.arange(table, dtype=jnp.int32)[:, None, None]
+    weights = jnp.sum(jnp.where(expert_ids[None] == numbers, gate_values[None].astype(F32), 0.0), axis=2)
+    anywhere = pl.BlockSpec(memory_space=pl.ANY)
+    shared_units = shared_gate.shape[1]
+    count = 18 * planes
+    return pl.pallas_call(
+        functools.partial(layer_kernel, lanes),
+        out_shape=jax.ShapeDtypeStruct((rows, narrow), BF16),
+        in_specs=[anywhere] * 8,
+        out_specs=pl.BlockSpec(memory_space=pltpu.VMEM),
+        scratch_shapes=[
+            pltpu.VMEM((tensors, lanes * rows, narrow), BF16),
+            pltpu.VMEM((lanes, table, rows), BF16),
+            pltpu.VMEM((features, quarter), BF16),
+            pltpu.VMEM((features, quarter), BF16),
+            pltpu.VMEM((quarter, features), BF16),
+            pltpu.VMEM((features, shared_units), BF16),
+            pltpu.VMEM((features, shared_units), BF16),
+            pltpu.VMEM((shared_units, features), BF16),
+            pltpu.VMEM((2 * rows, shared_units), BF16),
+            pltpu.VMEM((planes, tensors, 2 * rows, narrow), BF16),
+            pltpu.VMEM((planes, 2, 2 * rows, narrow), BF16),
+            pltpu.VMEM((planes, rows // 2, narrow), BF16),
+            pltpu.VMEM((planes, rows // 2, narrow), BF16),
+            pltpu.VMEM((planes, rows, narrow), BF16),
+            pltpu.VMEM((planes, rows, narrow), BF16),
+            pltpu.VMEM((planes, rows, narrow), BF16),
+            pltpu.SemaphoreType.DMA((8,)),
+            pltpu.SemaphoreType.DMA((count,)),
+            pltpu.SemaphoreType.DMA((count,)),
+        ],
+        compiler_params=pltpu.CompilerParams(
+            collective_id=0, has_side_effects=True, vmem_limit_bytes=60 * 1024 * 1024
+        ),
+    )(tokens, weights.astype(BF16), w_gate[0], w_up[0], w_down[0], shared_gate, shared_up, shared_down)
+
+
+def per_device(tokens, expert_ids, gate_values, w_gate, *rest):
+    per_lane = w_gate.shape[0]
+    lanes, tensors = lax.axis_size("expert"), lax.axis_size("tensor")
+    top = expert_ids.shape[1]
+    capacity = capacity_of(tokens.shape[0], top, lanes * per_lane)
+    grouped = per_lane == 1 and tensors == 4 and lanes % 2 == 0 and lanes >= 8
+    dense = grouped and 2 * capacity >= tokens.shape[0]
+    form = kernel_form if dense else dispatch_form
+    return form(tokens, expert_ids, gate_values, w_gate, *rest)
+
+
 def solution(mesh):
     placed = (
         P("expert", "tensor"),

time: 258 us -> 80 us (0.31)
  waiting for transfers between devices: 107 us -> 0 us
  Pallas kernels: 0 us -> 76.2 us
  blocking collectives: 49.9 us -> 0 us
  local copies, waits for them, and re-layouts: 49.8 us -> 1.65 us
  matrix products: 22.1 us -> 0 us
  between operations: 13.2 us -> 0.01 us
  other arithmetic: 8.93 us -> 1.97 us
  starting transfers between devices: 5.77 us -> 0 us
    pallas_call x0 -> x1, Pallas kernels: none -> 76.2 us  [kernel_form(): pl.pallas_call(functools.partial(layer_kernel, lanes), out_shape=jax.Shap...]
    unnamed x5 -> x0, waiting for transfers between devices: 67.1 us -> none
    all_to_all x1 -> x0, blocking collectives: 40.6 us -> none  [per_device(): lax.all_to_all(outgoing, 'expert', split_axis=0, concat_axis=0, tiled=True)]
    all_gather x1 -> x0, waiting for transfers between devices: 40.4 us -> none  [per_device(): block_rows = lax.all_gather(arrived, 'tensor', axis=3, tiled=True)]
    unnamed x12 -> x1, local copies, waits for them, and re-layouts: 34.9 us -> 1.65 us
    dot_general x4 -> x0, matrix products: 22.1 us -> none  [the longest x1 11.3 us: per_device(): jnp.einsum('sjcf,jfd->sjcd', hidden, w_down, preferred_element_type=jnp.f...]
    gather x3 -> x0, local copies, waits for them, and re-layouts: 10.7 us -> none  [the longest x2 7.93 us: per_device(): picked = returned.reshape(total_rows, narrow)[target]]
    all_gather x1 -> x0, blocking collectives: 9.36 us -> none  [per_device(): features_all = lax.all_gather(tokens, 'tensor', axis=1, tiled=True)]
  transfers between devices with their start and end apart: 4 -> 0, of which waited for: 3 -> 0; matrix products, arithmetic and copies ran while one was open for 4% -> 0% of each run, Pallas kernels for 0% -> 0%
where the time goes in v1:
time: 80 us; the launch traced here: 79.8 us
  Pallas kernels  76.2 us (95%)
  other arithmetic  1.97 us (2%)
  local copies, waits for them, and re-layouts  1.65 us (2%)
    pallas_call x1, Pallas kernels, kernel_form(): pl.pallas_call(functools.partial(layer_kernel, lanes), out_shape=jax.Shap...  76.2 us
    unnamed x1, local copies, waits for them, and re-layouts  1.65 us

profile of v1, /device:TPU:0, one launch (start us, length us, event | category | flops | bytes accessed | tf_op | source)
XLA Modules:
  0.0 79.8 jit_solution(16980663176017538149)
XLA Ops:
  0.0 0.7 convert_element_type.7
  0.7 1.3 %select_reduce_fusion.wt_hbm = bf16[16,128]{1,0:T(8,128)(2,1)} fusion(f32[128,4]{0,1:T(4,128)S(1)} %convert_element_type.7, s32[128,4]{0,1:T(4,128)} %param.10), kind=kLoop, calls=%fused_computation | loop fusion | flops 22528 | bytes 8192 | tf_op jit(solution)/shard_map/reduce_sum | solution.py:306
  2.0 76.2 %shard_map.91 = bf16[128,896]{1,0:T(8,128)(2,1)} custom-call(bf16[128,896]{1,0:T(8,128)(2,1)} %tok_hbm.1, bf16[16,128]{1,0:T(8,128)(2,1)} %select_reduce_fusion.wt_hbm, bf16[3584,256]{1,0:T(8,128)(2,1)} %bitcast.3, bf16[3584,256]{1,0:T(8,128)(2,1)} %bitcast.4, bf16[256,3584]{1,0:T(8,128)(2,1)} %bitcast.5, bf16[3584,256]{1,0:T(8,128)(2,1)} %sg_hbm.1, ...), custom_call_target="tpu_custom_call" | custom-call | tf_op jit(solution)/shard_map/pallas_call | solution.py:310
  78.2 1.6 %copy.13 = bf16[128,896]{1,0:T(8,128)(2,1)} copy(bf16[128,896]{1,0:T(8,128)(2,1)} %shard_map.91) | data formatting | bytes 458752

commit v2 on v1

--- a/solution.py
+++ b/solution.py
@@ -69,7 +69,7 @@
 def layer_kernel(
     lanes, tok_hbm, wt_hbm, wg_hbm, wu_hbm, wd_hbm, sg_hbm, su_hbm, sd_hbm, out_ref,
     xbuf, wtb, wg, wu, wd, sg, su, sd, shared_hidden, part, got_core, got_h0, got_h1,
-    got_x, got_y, got_z, load_sem, send_sem, recv_sem,
+    got_x, got_y, got_z, got_far, load_sem, send_sem, recv_sem,
 ):
     planes = lanes // 2
     rows, narrow = out_ref.shape
@@ -88,6 +88,8 @@
     at_down = (down * 2 + x, tens)
     tens_y = oy * 2 + c
     number, copies = {}, {}
+    gather_ring = range(planes - 2, planes)
+    reduce_ring_far = range(0)
 
     def send(key, src, dst, device):
         k = number.setdefault(key, len(number))
@@ -137,29 +139,40 @@
         if s < planes - 1:
             send(("z", s), mine, mine, at_up)
             send(("wz", s), weight, weight, at_up)
-        send(("x", s), mine, mine, at_x)
-        send(("y", s), mine, mine, at_y)
+        for h in range(2):
+            ahead, behind = half_piece(tens, p, x, h), half_piece(tens, p, x, 1 - h)
+            send(("x", h, s), ahead, ahead, at_x)
+            send(("y", 1 - h, s), behind, behind, at_y)
         send(("wx", s), weight, weight, at_x)
         send(("c", s), mine, mine, at_core)
 
     def forward(s):
         p = plane_at(s)
-        arrived(("x", s))
-        first = half_piece(tens, p, ox, 0)
-        send(("d0", s), first, first, at_y)
+        arrived(("x", 0, s))
+        if s not in gather_ring:
+            first = half_piece(tens, p, ox, 0)
+            send(("d0", s), first, first, at_y)
+        arrived(("y", 1, s))
+        if s not in gather_ring:
+            second = half_piece(tens_y, p, x, 1)
+            send(("d1", s), second, second, at_x)
+        arrived(("x", 1, s))
         other = piece(tens, p, ox)
         send(("cx", s), other, other, at_core)
-        arrived(("y", s))
-        second = half_piece(tens_y, p, x, 1)
-        send(("d1", s), second, second, at_x)
+        arrived(("y", 0, s))
         other = piece(tens_y, p, x)
         send(("cy", s), other, other, at_core)
 
     def finish(s):
         p = plane_at(s)
-        arrived(("d0", s))
-        arrived(("d1", s))
         far = piece(tens_y, p, ox)
+        if s in gather_ring:
+            arrived(("zd", s - 1))
+        else:
+            arrived(("d0", s))
+            arrived(("d1", s))
+        if s + 1 in gather_ring:
+            send(("zd", s), far, far, at_up)
         send(("cd", s), far, far, at_core)
         arrived(("wx", s))
         for key in ("c", "cx", "cy", "cd"):
@@ -227,20 +240,29 @@
 
         side(oy, ox)
         far = sum_piece(s, oy, ox)
-        send(("r0", s), far.at[0:half, :], got_h0.at[s], at_y)
-        send(("r1", s), far.at[half:rows, :], got_h1.at[s], at_x)
+        previous = planes - 1 if s == 0 else s - 1
+        if previous in reduce_ring_far:
+            arrived(("zf", previous))
+            add(rows, far, got_far.at[previous])
+        if s in reduce_ring_far:
+            send(("zf", s), far, got_far.at[s], at_up)
+        else:
+            send(("r0", s), far.at[0:half, :], got_h0.at[s], at_y)
+            send(("r1", s), far.at[half:rows, :], got_h1.at[s], at_x)
         side(y, ox)
         side(oy, x)
         side(y, x)
 
     def reduce_near(s):
-        arrived(("r0", s))
         aside = sum_piece(s, y, ox)
-        add(half, aside.at[0:half, :], got_h0.at[s])
+        if s not in reduce_ring_far:
+            arrived(("r0", s))
+            add(half, aside.at[0:half, :], got_h0.at[s])
         send(("rx", s), aside, got_x.at[s], at_x)
-        arrived(("r1", s))
         across = sum_piece(s, oy, x)
-        add(half, across.at[half:rows, :], got_h1.at[s])
+        if s not in reduce_ring_far:
+            arrived(("r1", s))
+            add(half, across.at[half:rows, :], got_h1.at[s])
         send(("ry", s), across, got_y.at[s], at_y)
 
     def reduce_ring(s, before):
@@ -306,7 +328,7 @@
     weights = jnp.sum(jnp.where(expert_ids[None] == numbers, gate_values[None].astype(F32), 0.0), axis=2)
     anywhere = pl.BlockSpec(memory_space=pl.ANY)
     shared_units = shared_gate.shape[1]
-    count = 18 * planes
+    count = 24 * planes
     return pl.pallas_call(
         functools.partial(layer_kernel, lanes),
         out_shape=jax.ShapeDtypeStruct((rows, narrow), BF16),
@@ -329,6 +351,7 @@
             pltpu.VMEM((planes, rows, narrow), BF16),
             pltpu.VMEM((planes, rows, narrow), BF16),
             pltpu.VMEM((planes, rows, narrow), BF16),
+            pltpu.VMEM((planes, rows, narrow), BF16),
             pltpu.SemaphoreType.DMA((8,)),
             pltpu.SemaphoreType.DMA((count,)),
             pltpu.SemaphoreType.DMA((count,)),

time: 80 us -> 74.8 us (0.935)
  Pallas kernels: 76.2 us -> 71 us
    pallas_call x1, Pallas kernels: 76.2 us -> 71 us  [kernel_form(): pl.pallas_call(functools.partial(layer_kernel, lanes), out_shape=jax.Shap...]
where the time goes in v2:
time: 74.8 us; the launch traced here: 74.6 us
  Pallas kernels  71 us (95%)
  other arithmetic  1.97 us (3%)
  local copies, waits for them, and re-layouts  1.65 us (2%)
    pallas_call x1, Pallas kernels, kernel_form(): pl.pallas_call(functools.partial(layer_kernel, lanes), out_shape=jax.Shap...  71 us
    unnamed x1, local copies, waits for them, and re-layouts  1.65 us

profile of v2, /device:TPU:0, one launch (start us, length us, event | category | flops | bytes accessed | tf_op | source)
XLA Modules:
  0.0 74.6 jit_solution(358122379347035921)
XLA Ops:
  0.0 0.7 convert_element_type.7
  0.7 1.3 %select_reduce_fusion.wt_hbm = bf16[16,128]{1,0:T(8,128)(2,1)} fusion(f32[128,4]{0,1:T(4,128)S(1)} %convert_element_type.7, s32[128,4]{0,1:T(4,128)} %param.10), kind=kLoop, calls=%fused_computation | loop fusion | flops 22528 | bytes 8192 | tf_op jit(solution)/shard_map/reduce_sum | solution.py:328
  2.0 71.0 %shard_map.91 = bf16[128,896]{1,0:T(8,128)(2,1)} custom-call(bf16[128,896]{1,0:T(8,128)(2,1)} %tok_hbm.1, bf16[16,128]{1,0:T(8,128)(2,1)} %select_reduce_fusion.wt_hbm, bf16[3584,256]{1,0:T(8,128)(2,1)} %bitcast.3, bf16[3584,256]{1,0:T(8,128)(2,1)} %bitcast.4, bf16[256,3584]{1,0:T(8,128)(2,1)} %bitcast.5, bf16[3584,256]{1,0:T(8,128)(2,1)} %sg_hbm.1, ...), custom_call_target="tpu_custom_call" | custom-call | tf_op jit(solution)/shard_map/pallas_call | solution.py:332
  72.9 1.6 %copy.13 = bf16[128,896]{1,0:T(8,128)(2,1)} copy(bf16[128,896]{1,0:T(8,128)(2,1)} %shard_map.91) | data formatting | bytes 458752

commit v3 on v2

--- a/solution.py
+++ b/solution.py
@@ -285,13 +285,15 @@
     if last:
         issue(1)
     finish(0)
+    forward(1)
+    issue(2)
     compute(0)
     reduce_core(0)
     for s in range(1, planes):
-        forward(s)
-        if s < last:
-            issue(s + 1)
         if s >= 2:
+            forward(s)
+            if s < last:
+                issue(s + 1)
             reduce_far(s - 1)
         if s >= 3:
             reduce_near(s - 2)

time: 74.8 us -> 73 us (0.976)
  Pallas kernels: 71 us -> 69.2 us
    pallas_call x1, Pallas kernels: 71 us -> 69.2 us  [kernel_form(): pl.pallas_call(functools.partial(layer_kernel, lanes), out_shape=jax.Shap...]
where the time goes in v3:
time: 73 us; the launch traced here: 72.8 us
  Pallas kernels  69.2 us (95%)
  other arithmetic  1.97 us (3%)
  local copies, waits for them, and re-layouts  1.65 us (2%)
    pallas_call x1, Pallas kernels, kernel_form(): pl.pallas_call(functools.partial(layer_kernel, lanes), out_shape=jax.Shap...  69.2 us
    unnamed x1, local copies, waits for them, and re-layouts  1.65 us

profile of v3, /device:TPU:0, one launch (start us, length us, event | category | flops | bytes accessed | tf_op | source)
XLA Modules:
  0.0 72.8 jit_solution(6704829453479417805)
XLA Ops:
  0.0 0.7 convert_element_type.7
  0.7 1.3 %select_reduce_fusion.wt_hbm = bf16[16,128]{1,0:T(8,128)(2,1)} fusion(f32[128,4]{0,1:T(4,128)S(1)} %convert_element_type.7, s32[128,4]{0,1:T(4,128)} %param.10), kind=kLoop, calls=%fused_computation | loop fusion | flops 22528 | bytes 8192 | tf_op jit(solution)/shard_map/reduce_sum | solution.py:330
  2.0 69.2 %shard_map.91 = bf16[128,896]{1,0:T(8,128)(2,1)} custom-call(bf16[128,896]{1,0:T(8,128)(2,1)} %tok_hbm.1, bf16[16,128]{1,0:T(8,128)(2,1)} %select_reduce_fusion.wt_hbm, bf16[3584,256]{1,0:T(8,128)(2,1)} %bitcast.3, bf16[3584,256]{1,0:T(8,128)(2,1)} %bitcast.4, bf16[256,3584]{1,0:T(8,128)(2,1)} %bitcast.5, bf16[3584,256]{1,0:T(8,128)(2,1)} %sg_hbm.1, ...), custom_call_target="tpu_custom_call" | custom-call | tf_op jit(solution)/shard_map/pallas_call | solution.py:334
  71.2 1.6 %copy.13 = bf16[128,896]{1,0:T(8,128)(2,1)} copy(bf16[128,896]{1,0:T(8,128)(2,1)} %shard_map.91) | data formatting | bytes 458752
